TPU v7x, 32 devices: a whole 2x2x4 slice. The times are simulated.
32 devices in a mesh: field: 8 (over y, x, core), slab: 4 (over z).
Axes of the slice: x: 2, y: 2, z: 4, core: 2. Of those that a mesh axis runs over, the one named last changes fastest.
Arguments:
- fields: float32 [32, 16, 16, 16, 128], P('field', None, 'slab'), may hold values from -6 to 6
- velocity: float32 [3, 16, 16, 128], P(None, 'slab'), may hold values from -0.15 to 0.15
- diffusivity: float32 [16, 16, 128], P('slab'), may hold values from 0.06 to 0.14
- noise: float32 [32, 4, 3], P('field'), may hold values from -0.8 to 0.8
- mix_rate: float32 [16, 16, 128], P('slab'), may hold values from 0.2 to 1
- evaporation: float32 [16, 16, 128], P('slab'), may hold values from 0.05 to 0.5
- rate_matrix: float32 [32, 16], replicated, may hold values from -1.5 to 1.5
- stoich: float32 [16, 32], replicated, may hold values from -1 to 1
- prefactor: float32 [32], replicated, may hold values from 0.05 to 0.5
Outputs:
- updated: float32 [32, 16, 16, 16, 128], P('field', None, 'slab')
All inputs are finite; a program needn't handle non-finite values.
Results may differ from a plain program's by a relative error of at most 0.000073.
Values sent between devices are 32-bit elements; how exact they have to be, the bound alone decides.
A program may use at most 64 MiB of HBM per device.

v0:
```python
import jax
import jax.numpy as jnp
from jax import lax
from jax.sharding import PartitionSpec as P

F = 32
SUBSTEPS = 4


def with_halo(cells, sides, width):
    for axis, dim in sides:
        count = lax.axis_size(axis)
        ends = count - 1
        head = lax.slice_in_dim(cells, 0, width, axis=dim)
        tail = lax.slice_in_dim(cells, cells.shape[dim] - width, cells.shape[dim], axis=dim)
        cells = jnp.concatenate(
            [
                lax.ppermute(tail, axis, [(i, (i + 1) % count) for i in range(ends)]),
                cells,
                lax.ppermute(head, axis, [((i + 1) % count, i) for i in range(ends)]),
            ],
            axis=dim,
        )
    return cells


def advance(padded, velocity, diffusivity, drifts):
    center = padded[:, :, 1:-1]
    x_ahead = padded[:, :, 2:]
    x_behind = padded[:, :, :-2]
    y_ahead = jnp.roll(center, -1, axis=4)
    y_behind = jnp.roll(center, 1, axis=4)
    z_ahead = jnp.roll(center, -1, axis=3)
    z_behind = jnp.roll(center, 1, axis=3)
    spread = x_ahead + x_behind + y_ahead + y_behind + z_ahead + z_behind - 6.0 * center
    stir_scale = jnp.sqrt(2.0 * diffusivity)
    drift_x = velocity[0] - stir_scale * drifts[:, 0][:, None, None, None, None]
    drift_y = velocity[1] - stir_scale * drifts[:, 1][:, None, None, None, None]
    drift_z = velocity[2] - stir_scale * drifts[:, 2][:, None, None, None, None]
    carried = (
        drift_x * (x_ahead - x_behind) * 0.5
        + drift_y * (y_ahead - y_behind) * 0.5
        + drift_z * (z_ahead - z_behind) * 0.5
    )
    return center + diffusivity * spread - carried


def react(states, average, rates, vapour, rate_matrix, stoich, prefactor):
    species = states.shape[1]
    fuel = (jnp.arange(species) == 0).astype(jnp.float32)
    mixed = states - 0.5 * rates * (states - average) + vapour * fuel[:, None]
    drive = jnp.einsum("rs,ksc->krc", rate_matrix, mixed, precision=lax.Precision.HIGHEST)
    speed = prefactor[None, :, None] * jnp.exp(2.0 * jnp.tanh(drive))
    return mixed + jnp.einsum("sr,krc->ksc", stoich, speed, precision=lax.Precision.HIGHEST)


def per_device(
    fields, velocity, diffusivity, noise, mix_rate, evaporation, rate_matrix, stoich, prefactor
):
    state = fields
    for substep in range(SUBSTEPS):
        padded = with_halo(state, (("slab", 2),), 1)
        state = advance(padded, velocity, diffusivity, noise[:, substep])
    count_fields = state.shape[0]
    species = state.shape[1]
    flattened = state.reshape(count_fields, species, -1)
    average = lax.psum(jnp.sum(flattened, axis=0), "field") / F
    reacted = react(
        flattened,
        average,
        mix_rate.reshape(-1),
        evaporation.reshape(-1),
        rate_matrix,
        stoich,
        prefactor,
    )
    return reacted.reshape(state.shape)


def solution(mesh):
    in_specs = (
        P("field", None, "slab", None, None),
        P(None, "slab", None, None),
        P("slab", None, None),
        P("field", None, None),
        P("slab", None, None),
        P("slab", None, None),
        P(),
        P(),
        P(),
    )
    out_specs = P("field", None, "slab", None, None)
    return jax.shard_map(
        per_device, mesh=mesh, in_specs=in_specs, out_specs=out_specs, check_vma=False
    )
```

profile of v0, /device:TPU:1, one launch (start us, length us, event | category | flops | bytes accessed | tf_op | source)
XLA Modules:
  0.0 165.6 jit_solution(18332196890247301672)
XLA Ops:
  6.5 2.4 %fusion.26 = (f32[4,16,1,16,128]{4,3,2,1,0:T(8,128)}, f32[4,16,1,16,128]{4,3,2,1,0:T(8,128)}) fusion(f32[4,16,4,16,128]{4,3,2,1,0:T(8,128)} %param.9), kind=kLoop, calls=%fused_computation.90 | loop fusion | bytes 2097152 | tf_op jit(solution)/shard_map/slice | solution.py:15
  9.0 1.3 collective-permute-start
  10.3 4.7 %collective-permute-start.1 = (f32[4,16,1,16,128]{4,3,2,1,0:T(8,128)}, f32[4,16,1,16,128]{4,3,2,1,0:T(8,128)S(1)}, u32[]{:S(2)}, u32[]{:S(2)}) collective-permute-start(f32[4,16,1,16,128]{4,3,2,1,0:T(8,128)} %get-tuple-element.49), channel_id=1, source_target_pairs={{0,1},{1,2},{2,3},{4,5},{5,6},{6,7},{8,9},{9,10},{10,11},{12,13},{... | collective-permute-start | bytes 1572872 | tf_op jit(solution)/shard_map/ppermute | solution.py:18
  15.0 2.9 %fusion.27 = (f32[4,16,4,16,127]{4,3,2,1,0:T(8,128)}, f32[4,16,4,16,127]{4,3,2,1,0:T(8,128)}) fusion(f32[4,16,4,16,128]{4,3,2,1,0:T(8,128)S(1)} %copy-done.1), kind=kLoop, calls=%fused_computation.91 | loop fusion | bytes 8323072 | tf_op jit(solution)/shard_map/jit(_roll_static)/slice | solution.py:31
  17.8 2.9 %fusion.28 = (f32[4,16,4,16,1]{4,3,2,1,0:T(8,128)}, f32[4,16,4,16,1]{4,3,2,1,0:T(8,128)}) fusion(f32[4,16,4,16,128]{4,3,2,1,0:T(8,128)S(1)} %copy-done.1), kind=kLoop, calls=%fused_computation.92 | loop fusion | bytes 65536 | tf_op jit(solution)/shard_map/jit(_roll_static)/slice | solution.py:31
  22.8 2.0 %collective-permute-done = f32[4,16,1,16,128]{4,3,2,1,0:T(8,128)S(1)} collective-permute-done((f32[4,16,1,16,128]{4,3,2,1,0:T(8,128)}, f32[4,16,1,16,128]{4,3,2,1,0:T(8,128)S(1)}, u32[]{:S(2)}, u32[]{:S(2)}) %collective-permute-start) | collective-permute-done | bytes 524320 | tf_op jit(solution)/shard_map/ppermute | solution.py:20
  24.8 1.0 collective-permute-done.1
  25.8 2.9 %multiply_subtract_fusion.3 = f32[4,16,4,16,128]{4,3,2,1,0:T(8,128)S(1)} fusion(f32[4,16,4,16,128]{4,3,2,1,0:T(8,128)S(1)} %copy-done.1, f32[4,16,4,15,128]{4,3,2,1,0:T(8,128)S(1)} %get-tuple-element.56, f32[4,16,4,1,128]{4,3,2,1,0:T(1,128)S(1)} %get-tuple-element.58, f32[4,16,4,1,128]{4,3,2,1,0:T(1,128)S(1)} %get-tuple-element.57, ...), kind=kLoop, calls=%fused_computation.35 | loop fusion | flops 13107200 | bytes 14057472 | tf_op jit(solution)/shard_map/sub | solution.py:45
  29.6 0.8 fusion.23
  30.6 1.3 collective-permute-start.2
  31.9 4.7 %collective-permute-start.3 = (f32[4,16,1,16,128]{4,3,2,1,0:T(8,128)S(1)}, f32[4,16,1,16,128]{4,3,2,1,0:T(8,128)S(1)}, u32[]{:S(2)}, u32[]{:S(2)}) collective-permute-start(f32[4,16,1,16,128]{4,3,2,1,0:T(8,128)S(1)} %get-tuple-element.39), channel_id=1, source_target_pairs={{0,1},{1,2},{2,3},{4,5},{5,6},{6,7},{8,9},{9,10},{10,11},{12,13},{... | collective-permute-start | bytes 1572872 | tf_op jit(solution)/shard_map/ppermute | solution.py:18
  37.4 7.9 %collective-permute-done.2 = f32[4,16,1,16,128]{4,3,2,1,0:T(8,128)S(1)} collective-permute-done((f32[4,16,1,16,128]{4,3,2,1,0:T(8,128)S(1)}, f32[4,16,1,16,128]{4,3,2,1,0:T(8,128)S(1)}, u32[]{:S(2)}, u32[]{:S(2)}) %collective-permute-start.2) | collective-permute-done | bytes 524320 | tf_op jit(solution)/shard_map/ppermute | solution.py:20
  45.4 0.9 collective-permute-done.3
  46.3 3.0 %multiply_subtract_fusion.2 = f32[4,16,4,16,128]{4,3,2,1,0:T(8,128)S(1)} fusion(f32[4,16,4,16,128]{4,3,2,1,0:T(8,128)S(1)} %multiply_subtract_fusion.3, f32[4,16,4,15,128]{4,3,2,1,0:T(8,128)S(1)} %get-tuple-element.46, f32[4,16,4,1,128]{4,3,2,1,0:T(1,128)S(1)} %get-tuple-element.48, f32[4,16,4,1,128]{4,3,2,1,0:T(1,128)S(1)} %get-tuple-element.47, ...), kind=kLoop, calls=%fused_computation.34 | loop fusion | flops 13107200 | bytes 14057472 | tf_op jit(solution)/shard_map/sub | solution.py:45
  50.1 0.8 fusion.18
  51.1 1.3 collective-permute-start.4
  52.4 4.9 %collective-permute-start.5 = (f32[4,16,1,16,128]{4,3,2,1,0:T(8,128)S(1)}, f32[4,16,1,16,128]{4,3,2,1,0:T(8,128)S(1)}, u32[]{:S(2)}, u32[]{:S(2)}) collective-permute-start(f32[4,16,1,16,128]{4,3,2,1,0:T(8,128)S(1)} %get-tuple-element.29), channel_id=1, source_target_pairs={{0,1},{1,2},{2,3},{4,5},{5,6},{6,7},{8,9},{9,10},{10,11},{12,13},{... | collective-permute-start | bytes 1572872 | tf_op jit(solution)/shard_map/ppermute | solution.py:18
  58.2 6.9 %collective-permute-done.4 = f32[4,16,1,16,128]{4,3,2,1,0:T(8,128)S(1)} collective-permute-done((f32[4,16,1,16,128]{4,3,2,1,0:T(8,128)S(1)}, f32[4,16,1,16,128]{4,3,2,1,0:T(8,128)S(1)}, u32[]{:S(2)}, u32[]{:S(2)}) %collective-permute-start.4) | collective-permute-done | bytes 524320 | tf_op jit(solution)/shard_map/ppermute | solution.py:20
  65.1 0.9 collective-permute-done.5
  66.0 2.9 %multiply_subtract_fusion.1 = f32[4,16,4,16,128]{4,3,2,1,0:T(8,128)S(1)} fusion(f32[4,16,4,16,128]{4,3,2,1,0:T(8,128)S(1)} %multiply_subtract_fusion.2, f32[4,16,4,15,128]{4,3,2,1,0:T(8,128)S(1)} %get-tuple-element.36, f32[4,16,4,1,128]{4,3,2,1,0:T(1,128)S(1)} %get-tuple-element.38, f32[4,16,4,1,128]{4,3,2,1,0:T(1,128)S(1)} %get-tuple-element.37, ...), kind=kLoop, calls=%fused_computation.33 | loop fusion | flops 13107200 | bytes 14057472 | tf_op jit(solution)/shard_map/sub | solution.py:45
  70.5 1.3 collective-permute-start.6
  71.8 4.8 %collective-permute-start.7 = (f32[4,16,1,16,128]{4,3,2,1,0:T(8,128)S(1)}, f32[4,16,1,16,128]{4,3,2,1,0:T(8,128)S(1)}, u32[]{:S(2)}, u32[]{:S(2)}) collective-permute-start(f32[4,16,1,16,128]{4,3,2,1,0:T(8,128)S(1)} %get-tuple-element.20), channel_id=1, source_target_pairs={{0,1},{1,2},{2,3},{4,5},{5,6},{6,7},{8,9},{9,10},{10,11},{12,13},{... | collective-permute-start | bytes 1572872 | tf_op jit(solution)/shard_map/ppermute | solution.py:18
  77.3 6.4 %collective-permute-done.6 = f32[4,16,1,16,128]{4,3,2,1,0:T(8,128)S(1)} collective-permute-done((f32[4,16,1,16,128]{4,3,2,1,0:T(8,128)S(1)}, f32[4,16,1,16,128]{4,3,2,1,0:T(8,128)S(1)}, u32[]{:S(2)}, u32[]{:S(2)}) %collective-permute-start.6) | collective-permute-done | bytes 524320 | tf_op jit(solution)/shard_map/ppermute | solution.py:20
  83.7 0.9 collective-permute-done.7
  84.6 3.9 %fusion.10 = (f32[16,4,16,128]{3,2,1,0:T(8,128)S(1)}, f32[4,16,4,16,128]{4,3,2,1,0:T(8,128)}) fusion(f32[4,4,16,128]{3,2,1,0:T(8,128)S(1)} %get-tuple-element.79, f32[4,4,16,128]{3,2,1,0:T(8,128)S(1)} %get-tuple-element.75, f32[4,4,16,128]{3,2,1,0:T(8,128)S(1)} %get-tuple-element.64, f32[4,16,4,16,128]{4,3,2,1,0:T(8,128)S(1)} %multiply_subtract_fusion.1, ...), kind=kLoop, calls=%fused_computation.74 | loop fusion | flops 13500416 | bytes 14581760 | tf_op jit(solution)/shard_map/reduce_sum | solution.py:67
  88.5 1.1 copy.21
  89.8 1.8 %reshape.150 = f32[4,16,8192]{2,1,0:T(8,128)S(1)} reshape(f32[4,16,4,16,128]{4,3,2,1,0:T(8,128)} %get-tuple-element.18) | data formatting | bytes 4194304 | tf_op jit(solution)/shard_map/reshape | solution.py:66
  91.5 57.2 %all-reduce.2.cloned.1.call-done = f32[16,8192]{1,0:T(8,128)} async-done(((f32[16,8192]{1,0:T(8,128)}), f32[16,8192]{1,0:T(8,128)}) %all-reduce.2.cloned.1.call-update) | async-done | bytes 524304 | tf_op jit(solution)/shard_map/psum | solution.py:67
  148.7 1.1 broadcast_multiply_fusion.1
  149.9 4.4 %fusion.3 = f32[4,32,8192]{2,1,0:T(8,128)S(1)} fusion(f32[32]{0:T(128)S(1)} %copy-done.12, f32[4,16,8192]{2,1,0:T(8,128)S(1)} %reshape.150, f32[16,8192]{1,0:T(8,128)S(1)} %broadcast_multiply_fusion, f32[16,8192]{1,0:T(8,128)S(1)} %broadcast_multiply_fusion.1, f32[8192]{0:T(1024)S(1)} %bitcast.39, f32[32,16]{0,1:T(8,128)S(1)} %copy-done), kind=kOutput, calls=%fused_computation.4 | convolution fusion | flops 205520896 | bytes 7374976 | tf_op jit(solution)/shard_map/rs,ksc->krc/dot_general | solution.py:52
  154.3 2.7 %fusion.4 = f32[4,16,8192]{2,1,0:T(8,128)S(1)} fusion(f32[4,32,8192]{2,1,0:T(8,128)S(1)} %fusion.3, f32[4,16,8192]{2,1,0:T(8,128)S(1)} %reshape.150, f32[16,8192]{1,0:T(8,128)S(1)} %broadcast_multiply_fusion, f32[16,8192]{1,0:T(8,128)S(1)} %broadcast_multiply_fusion.1, f32[8192]{0:T(1024)S(1)} %bitcast.40, f32[16,32]{1,0:T(8,128)S(1)} %copy-done.11), kind=kOutput, calls=%fused_computation.6 | convolution fusion | flops 203948032 | bytes 9472000 | tf_op jit(solution)/shard_map/sr,krc->ksc/dot_general | solution.py:54
  157.0 1.7 %copy.19 = f32[8,8,64,128]{3,2,1,0:T(8,128)} copy(f32[8,8,64,128]{3,1,2,0:T(8,128)S(1)} %bitcast.36) | data formatting | bytes 4194304
  (56 shorter events, 8.0 us)
Async XLA Ops:
  6.5 143.3 %copy-start = (f32[32,16]{0,1:T(8,128)S(1)}, f32[32,16]{0,1:T(8,128)}, u32[]{:S(2)}) copy-start(f32[32,16]{0,1:T(8,128)} %param.15) | copy-start | bytes 6148
  6.5 8.4 %copy-start.1 = (f32[4,16,4,16,128]{4,3,2,1,0:T(8,128)S(1)}, f32[4,16,4,16,128]{4,3,2,1,0:T(8,128)}, u32[]{:S(2)}) copy-start(f32[4,16,4,16,128]{4,3,2,1,0:T(8,128)} %param.9) | copy-start | bytes 6291460
  6.5 142.2 %all-reduce.2.cloned.1.call-start = ((), (), s32[]{:S(2)}) async-start(), calls=%async_computation | async-start | bytes 1048576 | tf_op jit(solution)/shard_map/psum | solution.py:67
  9.0 15.8 %collective-permute-start = (f32[4,16,1,16,128]{4,3,2,1,0:T(8,128)}, f32[4,16,1,16,128]{4,3,2,1,0:T(8,128)S(1)}, u32[]{:S(2)}, u32[]{:S(2)}) collective-permute-start(f32[4,16,1,16,128]{4,3,2,1,0:T(8,128)} %get-tuple-element.50), channel_id=1, source_target_pairs={{1,0},{2,1},{3,2},{5,4},{6,5},{7,6},{9,8},{10,9},{11,10},{13,12},{... | collective-permute-start | bytes 1572872 | tf_op jit(solution)/shard_map/ppermute | solution.py:20
  10.3 15.6 %collective-permute-start.1 = (f32[4,16,1,16,128]{4,3,2,1,0:T(8,128)}, f32[4,16,1,16,128]{4,3,2,1,0:T(8,128)S(1)}, u32[]{:S(2)}, u32[]{:S(2)}) collective-permute-start(f32[4,16,1,16,128]{4,3,2,1,0:T(8,128)} %get-tuple-element.49), channel_id=1, source_target_pairs={{0,1},{1,2},{2,3},{4,5},{5,6},{6,7},{8,9},{9,10},{10,11},{12,13},{... | collective-permute-start | bytes 1572872 | tf_op jit(solution)/shard_map/ppermute | solution.py:18
  17.8 2.9 %copy-start.8 = (f32[4,4,3]{1,0,2:T(4,128)S(1)}, f32[4,4,3]{1,0,2:T(4,128)}, u32[]{:S(2)}) copy-start(f32[4,4,3]{1,0,2:T(4,128)} %param.12) | copy-start | bytes 580
  17.8 3.4 %copy-start.7 = (f32[3,4,16,128]{3,2,1,0:T(8,128)S(1)}, f32[3,4,16,128]{3,2,1,0:T(8,128)}, u32[]{:S(2)}) copy-start(f32[3,4,16,128]{3,2,1,0:T(8,128)} %param.10) | copy-start | bytes 294916
  17.8 3.4 %copy-start.6 = (f32[4,16,128]{2,1,0:T(8,128)S(1)}, f32[4,16,128]{2,1,0:T(8,128)}, u32[]{:S(2)}) copy-start(f32[4,16,128]{2,1,0:T(8,128)} %param.11) | copy-start | bytes 98308
  22.2 3.6 %copy-start.2 = (f32[4,16,4,16,127]{4,3,2,1,0:T(8,128)S(1)}, f32[4,16,4,16,127]{4,3,2,1,0:T(8,128)}, u32[]{:S(2)}) copy-start(f32[4,16,4,16,127]{4,3,2,1,0:T(8,128)} %get-tuple-element.51) | copy-start | bytes 6242308
  22.2 3.6 %copy-start.3 = (f32[4,16,4,16,127]{4,3,2,1,0:T(8,128)S(1)}, f32[4,16,4,16,127]{4,3,2,1,0:T(8,128)}, u32[]{:S(2)}) copy-start(f32[4,16,4,16,127]{4,3,2,1,0:T(8,128)} %get-tuple-element.52) | copy-start | bytes 6242308
  22.2 3.6 %copy-start.4 = (f32[4,16,4,16,1]{4,3,2,1,0:T(8,128)S(1)}, f32[4,16,4,16,1]{4,3,2,1,0:T(8,128)}, u32[]{:S(2)}) copy-start(f32[4,16,4,16,1]{4,3,2,1,0:T(8,128)} %get-tuple-element.53) | copy-start | bytes 49156
  22.2 3.6 %copy-start.5 = (f32[4,16,4,16,1]{4,3,2,1,0:T(8,128)S(1)}, f32[4,16,4,16,1]{4,3,2,1,0:T(8,128)}, u32[]{:S(2)}) copy-start(f32[4,16,4,16,1]{4,3,2,1,0:T(8,128)} %get-tuple-element.54) | copy-start | bytes 49156
  30.6 14.8 %collective-permute-start.2 = (f32[4,16,1,16,128]{4,3,2,1,0:T(8,128)S(1)}, f32[4,16,1,16,128]{4,3,2,1,0:T(8,128)S(1)}, u32[]{:S(2)}, u32[]{:S(2)}) collective-permute-start(f32[4,16,1,16,128]{4,3,2,1,0:T(8,128)S(1)} %get-tuple-element.40), channel_id=1, source_target_pairs={{1,0},{2,1},{3,2},{5,4},{6,5},{7,6},{9,8},{10,9},{11,10},{13,12},{... | collective-permute-start | bytes 1572872 | tf_op jit(solution)/shard_map/ppermute | solution.py:20
  31.9 14.4 %collective-permute-start.3 = (f32[4,16,1,16,128]{4,3,2,1,0:T(8,128)S(1)}, f32[4,16,1,16,128]{4,3,2,1,0:T(8,128)S(1)}, u32[]{:S(2)}, u32[]{:S(2)}) collective-permute-start(f32[4,16,1,16,128]{4,3,2,1,0:T(8,128)S(1)} %get-tuple-element.39), channel_id=1, source_target_pairs={{0,1},{1,2},{2,3},{4,5},{5,6},{6,7},{8,9},{9,10},{10,11},{12,13},{... | collective-permute-start | bytes 1572872 | tf_op jit(solution)/shard_map/ppermute | solution.py:18
  51.1 14.0 %collective-permute-start.4 = (f32[4,16,1,16,128]{4,3,2,1,0:T(8,128)S(1)}, f32[4,16,1,16,128]{4,3,2,1,0:T(8,128)S(1)}, u32[]{:S(2)}, u32[]{:S(2)}) collective-permute-start(f32[4,16,1,16,128]{4,3,2,1,0:T(8,128)S(1)} %get-tuple-element.30), channel_id=1, source_target_pairs={{1,0},{2,1},{3,2},{5,4},{6,5},{7,6},{9,8},{10,9},{11,10},{13,12},{... | collective-permute-start | bytes 1572872 | tf_op jit(solution)/shard_map/ppermute | solution.py:20
  52.4 13.6 %collective-permute-start.5 = (f32[4,16,1,16,128]{4,3,2,1,0:T(8,128)S(1)}, f32[4,16,1,16,128]{4,3,2,1,0:T(8,128)S(1)}, u32[]{:S(2)}, u32[]{:S(2)}) collective-permute-start(f32[4,16,1,16,128]{4,3,2,1,0:T(8,128)S(1)} %get-tuple-element.29), channel_id=1, source_target_pairs={{0,1},{1,2},{2,3},{4,5},{5,6},{6,7},{8,9},{9,10},{10,11},{12,13},{... | collective-permute-start | bytes 1572872 | tf_op jit(solution)/shard_map/ppermute | solution.py:18
  70.5 13.2 %collective-permute-start.6 = (f32[4,16,1,16,128]{4,3,2,1,0:T(8,128)S(1)}, f32[4,16,1,16,128]{4,3,2,1,0:T(8,128)S(1)}, u32[]{:S(2)}, u32[]{:S(2)}) collective-permute-start(f32[4,16,1,16,128]{4,3,2,1,0:T(8,128)S(1)} %get-tuple-element.19), channel_id=1, source_target_pairs={{1,0},{2,1},{3,2},{5,4},{6,5},{7,6},{9,8},{10,9},{11,10},{13,12},{... | collective-permute-start | bytes 1572872 | tf_op jit(solution)/shard_map/ppermute | solution.py:20
  71.8 12.8 %collective-permute-start.7 = (f32[4,16,1,16,128]{4,3,2,1,0:T(8,128)S(1)}, f32[4,16,1,16,128]{4,3,2,1,0:T(8,128)S(1)}, u32[]{:S(2)}, u32[]{:S(2)}) collective-permute-start(f32[4,16,1,16,128]{4,3,2,1,0:T(8,128)S(1)} %get-tuple-element.20), channel_id=1, source_target_pairs={{0,1},{1,2},{2,3},{4,5},{5,6},{6,7},{8,9},{9,10},{10,11},{12,13},{... | collective-permute-start | bytes 1572872 | tf_op jit(solution)/shard_map/ppermute | solution.py:18
  84.6 5.0 %copy-start.9 = (f32[4,16,128]{2,1,0:T(8,128)S(1)}, f32[4,16,128]{2,1,0:T(8,128)}, u32[]{:S(2)}) copy-start(f32[4,16,128]{2,1,0:T(8,128)} %param.14) | copy-start | bytes 98308
  88.5 1.3 copy-start.10
  89.8 60.1 %copy-start.12 = (f32[32]{0:T(128)S(1)}, f32[32]{0:T(128)}, u32[]{:S(2)}) copy-start(f32[32]{0:T(128)} %param.17) | copy-start | bytes 388
  149.8 4.5 %copy-start.11 = (f32[16,32]{1,0:T(8,128)S(1)}, f32[16,32]{1,0:T(8,128)}, u32[]{:S(2)}) copy-start(f32[16,32]{1,0:T(8,128)} %param.16) | copy-start | bytes 6148
Sparse Core Ops, SparseCore 0:
  89.7 58.9 all-reduce.1
where the time goes:
time: 167 us; the launch traced here: 166 us
  waiting for transfers between devices  84.2 us (50%)
  starting transfers between devices  24.2 us (14%)
  local copies, waits for them, and re-layouts  22.1 us (13%)
  other arithmetic  14.2 us (9%)
  between operations  13.8 us (8%)
  matrix products  7.13 us (4%)
    psum x1, waiting for transfers between devices, per_device(): average = lax.psum(jnp.sum(flattened, axis=0), 'field') / F  57.2 us
    ppermute x4, waiting for transfers between devices, with_halo(): lax.ppermute(head, axis, [((i + 1) % count, i) for i in range(ends)])  23.2 us
    ppermute x4, starting transfers between devices, with_halo(): lax.ppermute(tail, axis, [(i, (i + 1) % count) for i in range(ends)])  19.1 us
    slice x8, local copies, waits for them, and re-layouts, advance(): y_ahead = jnp.roll(center, -1, axis=4)  10.6 us
    sub x3, other arithmetic, advance(): return center + diffusivity * spread - carried  8.86 us
    ppermute x4, starting transfers between devices, with_halo(): lax.ppermute(head, axis, [((i + 1) % count, i) for i in range(ends)])  5.16 us
    dot_general x1, matrix products, react(): jnp.einsum('rs,ksc->krc', rate_matrix, mixed, precision=lax.Precision.HIG...  4.43 us
    reduce_sum x1, other arithmetic, per_device(): average = lax.psum(jnp.sum(flattened, axis=0), 'field') / F  3.9 us
  transfers between devices with their start and end apart: 9, of which 9 were waited for; matrix products, arithmetic and copies ran while one was open for 7% of the time, Pallas kernels for 0%

commit v1 on v0

v1 whole, which is shorter than its diff:
```python
import functools

import jax
import jax.numpy as jnp
from jax import lax
from jax.experimental import pallas as pl
from jax.experimental.pallas import tpu as pltpu
from jax.sharding import PartitionSpec as P

GROUP = 2
LANES = 4
DELAYS = (2, 2, 2, 2, 2, 2, 2)
ROWS = 8


def schedule(groups, substeps, stages):
    width = min(LANES, groups)
    events = []
    slot = 0
    for first in range(0, groups, width):
        wave = range(first, min(first + width, groups))
        for k in range(substeps):
            for g in wave:
                events.append((slot, 1, "move", g, k))
                if k == substeps - 1:
                    when = slot
                    for stage in range(stages):
                        when += DELAYS[stage % len(DELAYS)]
                        events.append((when, 0, "sum", g, stage))
                slot += 1
    return width, [e[2:] for e in sorted(events, key=lambda e: (e[0], e[1]))]


def expand(small, row_of, col_of):
    rows, cols = small.shape
    tall = lax.broadcasted_iota(jnp.int32, (rows * ROWS, rows), 0) // ROWS
    pick_row = (tall == lax.broadcasted_iota(jnp.int32, (rows * ROWS, rows), 1)).astype(jnp.bfloat16)
    wide = lax.broadcasted_iota(jnp.int32, (cols, cols * ROWS), 1) // ROWS
    pick_col = (wide == lax.broadcasted_iota(jnp.int32, (cols, cols * ROWS), 0)).astype(jnp.bfloat16)
    half = jnp.dot(pick_row, small, preferred_element_type=jnp.float32).astype(jnp.bfloat16)
    full = jnp.dot(half, pick_col, preferred_element_type=jnp.float32)
    shape = (rows * ROWS, cols * ROWS)
    same = (lax.broadcasted_iota(jnp.int32, shape, 0) % ROWS) == (
        lax.broadcasted_iota(jnp.int32, shape, 1) % ROWS
    )
    return jnp.where(same, full, 0.0).astype(jnp.bfloat16)


def halves(value):
    high = value.astype(jnp.bfloat16)
    low = (value - high.astype(jnp.float32)).astype(jnp.bfloat16)
    return high, low


def kernel(
    slabs, peers, substeps,
    x_hbm, vel, diff, noise, rate, vapour, matrix, stoich, pref,
    out_hbm,
    st, halo, planes, part, got, acc, tot, xs, outv, a_one, a_two, b_all,
    in_sem, out_sem, hs_sem, hr_sem, rs_sem, rr_sem,
):
    fields, species, nx, nz, ny = x_hbm.shape
    reactions = matrix.shape[0]
    groups = species // GROUP
    bits = peers.bit_length() - 1
    stages = bits + 1
    half = nx // 2
    total_fields = fields * peers
    blocks = nz // ROWS

    def members(g):
        return pl.ds(g * GROUP, GROUP)

    loads = [
        pltpu.make_async_copy(x_hbm.at[:, members(g)], st.at[0, :, members(g)], in_sem.at[g])
        for g in range(groups)
    ]
    for load in loads:
        load.start()

    me = lax.axis_index("slab")
    seat = lax.axis_index("field")

    def partner(bit):
        step = 1 << bit
        return seat + step * (1 - 2 * ((seat // step) % 2))

    core = seat % 2
    mine = pl.ds(core * half, half)
    theirs = pl.ds((1 - core) * half, half)

    barrier = pltpu.get_barrier_semaphore()

    @pl.when(me > 0)
    def _():
        pl.semaphore_signal(barrier, inc=1, device_id={"slab": me - 1})

    @pl.when(me < slabs - 1)
    def _():
        pl.semaphore_signal(barrier, inc=1, device_id={"slab": me + 1})

    for bit in range(bits):
        pl.semaphore_signal(barrier, inc=1, device_id={"field": partner(bit)})
    has_left = (me + slabs - 1) // slabs
    has_right = 1 - (me + 1) // slabs
    pl.semaphore_wait(barrier, bits + has_left + has_right)

    def to_left(g, k):
        source = x_hbm.at[:, members(g), 0] if k == 0 else st.at[k, :, members(g), 0]
        return pltpu.make_async_remote_copy(
            src_ref=source, dst_ref=halo.at[k, 1, :, members(g)],
            send_sem=hs_sem.at[k, 0, g], recv_sem=hr_sem.at[k, 1, g],
            device_id={"slab": me - 1},
        )

    def to_right(g, k):
        source = x_hbm.at[:, members(g), nx - 1] if k == 0 else st.at[k, :, members(g), nx - 1]
        return pltpu.make_async_remote_copy(
            src_ref=source, dst_ref=halo.at[k, 0, :, members(g)],
            send_sem=hs_sem.at[k, 1, g], recv_sem=hr_sem.at[k, 0, g],
            device_id={"slab": me + 1},
        )

    def send_halo(g, k):
        @pl.when(me > 0)
        def _():
            to_left(g, k).start()

        @pl.when(me < slabs - 1)
        def _():
            to_right(g, k).start()

    def wait_halo(g, k):
        @pl.when(me > 0)
        def _():
            to_right(g, k).wait_recv()

        @pl.when(me < slabs - 1)
        def _():
            to_left(g, k).wait_recv()

    width, events = schedule(groups, substeps, stages)
    for g in range(width):
        send_halo(g, 0)

    @pl.when(me == 0)
    def _():
        for k in range(substeps):
            @pl.loop(0, fields)
            def _(f):
                halo[k, 0, f] = jnp.zeros((species, nz, ny), jnp.float32)

    @pl.when(me == slabs - 1)
    def _():
        for k in range(substeps):
            @pl.loop(0, fields)
            def _(f):
                halo[k, 1, f] = jnp.zeros((species, nz, ny), jnp.float32)

    for x in range(nx):
        d = diff[x]
        for i in range(3):
            planes[x, i] = d - 0.5 * vel[i, x]
        planes[x, 3] = 0.5 * jnp.sqrt(2.0 * d)
        planes[x, 4] = 2.0 * d
        planes[x, 5] = 1.0 - 6.0 * d

    w_high, w_low = halves(matrix[...])
    a_high = expand(w_high, ROWS, ROWS)
    a_one[...] = jnp.concatenate([a_high, a_high], axis=1)
    a_two[...] = expand(w_low, ROWS, ROWS)
    s_high, s_low = halves(stoich[...] * pref[...])
    b_high = expand(s_high, ROWS, ROWS)
    b_all[...] = jnp.concatenate([b_high, b_high, expand(s_low, ROWS, ROWS)], axis=1)

    def exchange(g, stage):
        if stage == 0:
            source, target, bit = part.at[members(g), theirs], got.at[0, members(g)], 0
        elif stage < bits:
            source, target, bit = acc.at[stage - 1, members(g)], got.at[stage, members(g)], stage
        else:
            source, target, bit = tot.at[members(g), mine], tot.at[members(g), mine], 0
        return pltpu.make_async_remote_copy(
            src_ref=source, dst_ref=target,
            send_sem=rs_sem.at[stage, g], recv_sem=rr_sem.at[stage, g],
            device_id={"field": partner(bit)},
        )

    def move(g, k):
        if k == 0:
            loads[g].wait()
        wait_halo(g, k)

        @pl.loop(0, fields)
        def _(f):
            shift = [noise[f, k, i] for i in range(3)]
            for x in range(nx):
                root = planes[x, 3]
                twice = planes[x, 4]
                diag = planes[x, 5]
                ahead = [planes[x, i] + root * shift[i] for i in range(3)]
                behind = [twice - a for a in ahead]
                for s in range(g * GROUP, (g + 1) * GROUP):
                    c = st[k, f, s, x]
                    xa = st[k, f, s, x + 1] if x + 1 < nx else halo[k, 1, f, s]
                    xb = st[k, f, s, x - 1] if x > 0 else halo[k, 0, f, s]
                    ya = pltpu.roll(c, ny - 1, 1)
                    yb = pltpu.roll(c, 1, 1)
                    za = pltpu.roll(c, nz - 1, 0)
                    zb = pltpu.roll(c, 1, 0)
                    st[k + 1, f, s, x] = (
                        (diag * c + (ahead[0] * xa + behind[0] * xb))
                        + (ahead[1] * ya + behind[1] * yb)
                        + (ahead[2] * za + behind[2] * zb)
                    )

        if k < substeps - 1:
            send_halo(g, k + 1)
            if k == substeps - 2 and g + width < groups:
                send_halo(g + width, 0)
        else:
            for s in range(g * GROUP, (g + 1) * GROUP):
                for x in range(nx):
                    part[s, x] = functools.reduce(
                        lambda a, b: a + b, [st[substeps, f, s, x] for f in range(fields)]
                    )
            exchange(g, 0).start()

    def mix(g):
        @pl.loop(0, fields)
        def _(f):
            for x in range(nx):
                half_rate = 0.5 * rate[x]
                for s in range(g * GROUP, (g + 1) * GROUP, 2):
                    pair = []
                    for one in (s, s + 1):
                        m = st[substeps, f, one, x]
                        m = m - half_rate * (m - tot[one, x] * (1.0 / total_fields))
                        if one == 0:
                            m = m + vapour[x]
                        outv[f, one, x] = m
                        pair.append(m)
                    for b in range(blocks):
                        rows = jnp.concatenate([m[b * ROWS:(b + 1) * ROWS] for m in pair], axis=0)
                        high, low = halves(rows)
                        lanes = slice(b * ny, (b + 1) * ny)
                        xs[f * nx + x, s * ROWS:(s + 2) * ROWS, lanes] = high
                        xs[f * nx + x, (species + s) * ROWS:(species + s + 2) * ROWS, lanes] = low

    def reduce_step(g, stage):
        exchange(g, stage).wait_recv()
        if stage == bits:
            mix(g)
            return
        for s in range(g * GROUP, (g + 1) * GROUP):
            held = part[s, mine] if stage == 0 else acc[stage - 1, s]
            value = held + got[stage, s]
            if stage == bits - 1:
                tot[s, mine] = value
            else:
                acc[stage, s] = value
        exchange(g, stage + 1).start()

    for kind, g, k in events:
        if kind == "move":
            move(g, k)
        else:
            reduce_step(g, k)

    def store(i):
        f, x = i // nx, i % nx
        return pltpu.make_async_copy(outv.at[f, :, x], out_hbm.at[f, :, x], out_sem.at[i])

    @pl.loop(0, fields * nx)
    def _(i):
        f, x = i // nx, i % nx
        drive = jnp.dot(a_one[...], xs[i], preferred_element_type=jnp.float32)
        drive = drive + jnp.dot(
            a_two[...], xs[i, : species * ROWS], preferred_element_type=jnp.float32
        )
        speed = jnp.exp(2.0 * jnp.tanh(drive))
        high, low = halves(speed)
        gain = jnp.dot(
            b_all[...], jnp.concatenate([high, low, high], axis=0),
            preferred_element_type=jnp.float32,
        )
        for b in range(blocks):
            piece = gain[:, b * ny:(b + 1) * ny].reshape(species, ROWS, ny)
            outv[f, :, x, b * ROWS:(b + 1) * ROWS] += piece
        store(i).start()

    for k in range(substeps):
        for g in range(groups):
            @pl.when(me > 0)
            def _():
                to_left(g, k).wait_send()

            @pl.when(me < slabs - 1)
            def _():
                to_right(g, k).wait_send()

    for g in range(groups):
        for stage in range(stages):
            exchange(g, stage).wait_send()

    @pl.loop(0, fields * nx)
    def _(i):
        store(i).wait()


def solution(mesh):
    slabs, peers = mesh.shape["slab"], mesh.shape["field"]

    def per_device(fields, velocity, diffusivity, noise, mix_rate, evaporation, rate_matrix, stoich, prefactor):
        count, species, nx, nz, ny = fields.shape
        substeps = noise.shape[1]
        reactions = rate_matrix.shape[0]
        groups = species // GROUP
        bits = peers.bit_length() - 1
        vmem = pl.BlockSpec(memory_space=pltpu.VMEM)
        f32, bf16 = jnp.float32, jnp.bfloat16
        dma = pltpu.SemaphoreType.DMA
        return pl.pallas_call(
            functools.partial(kernel, slabs, peers, substeps),
            out_shape=jax.ShapeDtypeStruct(fields.shape, f32),
            in_specs=[
                pl.BlockSpec(memory_space=pl.ANY), vmem, vmem,
                pl.BlockSpec(memory_space=pltpu.SMEM), vmem, vmem, vmem, vmem, vmem,
            ],
            out_specs=pl.BlockSpec(memory_space=pl.ANY),
            scratch_shapes=[
                pltpu.VMEM((substeps + 1, count, species, nx, nz, ny), f32),
                pltpu.VMEM((substeps, 2, count, species, nz, ny), f32),
                pltpu.VMEM((nx, 6, nz, ny), f32),
                pltpu.VMEM((species, nx, nz, ny), f32),
                pltpu.VMEM((bits, species, nx // 2, nz, ny), f32),
                pltpu.VMEM((bits, species, nx // 2, nz, ny), f32),
                pltpu.VMEM((species, nx, nz, ny), f32),
                pltpu.VMEM((count * nx, 2 * species * ROWS, (nz // ROWS) * ny), bf16),
                pltpu.VMEM((count, species, nx, nz, ny), f32),
                pltpu.VMEM((reactions * ROWS, 2 * species * ROWS), bf16),
                pltpu.VMEM((reactions * ROWS, species * ROWS), bf16),
                pltpu.VMEM((species * ROWS, 3 * reactions * ROWS), bf16),
                dma((groups,)),
                dma((count * nx,)),
                dma((substeps, 2, groups)),
                dma((substeps, 2, groups)),
                dma((bits + 1, groups)),
                dma((bits + 1, groups)),
            ],
            compiler_params=pltpu.CompilerParams(
                collective_id=0, has_side_effects=True, vmem_limit_bytes=60 * 1024 * 1024
            ),
        )(
            fields, velocity, diffusivity, noise, mix_rate, evaporation,
            rate_matrix, stoich, prefactor.reshape(1, -1),
        )

    in_specs = (
        P("field", None, "slab", None, None),
        P(None, "slab", None, None),
        P("slab", None, None),
        P("field", None, None),
        P("slab", None, None),
        P("slab", None, None),
        P(),
        P(),
        P(),
    )
    out_specs = P("field", None, "slab", None, None)
    return jax.shard_map(
        per_device, mesh=mesh, in_specs=in_specs, out_specs=out_specs, check_vma=False
    )
```

time: 167 us -> 80.8 us (0.48)
  waiting for transfers between devices: 84.2 us -> 0 us
  Pallas kernels: 0 us -> 74.6 us
  starting transfers between devices: 24.2 us -> 0 us
  local copies, waits for them, and re-layouts: 22.1 us -> 5.92 us
  other arithmetic: 14.2 us -> 0 us
  between operations: 13.8 us -> 0.01 us
  matrix products: 7.13 us -> 0 us
    pallas_call x0 -> x1, Pallas kernels: none -> 74.6 us  [per_device(): pl.pallas_call(functools.partial(kernel, slabs, peers, substeps), out_sha...]
    psum x1 -> x0, waiting for transfers between devices: 57.2 us -> none  [per_device(): average = lax.psum(jnp.sum(flattened, axis=0), 'field') / F]
    ppermute x8 -> x0, waiting for transfers between devices: 26.9 us -> none  [the longest x4 23.2 us: with_halo(): lax.ppermute(head, axis, [((i + 1) % count, i) for i in range(ends)])]
    ppermute x8 -> x0, starting transfers between devices: 24.2 us -> none  [the longest x4 19.1 us: with_halo(): lax.ppermute(tail, axis, [(i, (i + 1) % count) for i in range(ends)])]
    slice x27 -> x0, local copies, waits for them, and re-layouts: 17.5 us -> none  [the longest x8 10.6 us: advance(): y_ahead = jnp.roll(center, -1, axis=4)]
    sub x4 -> x0, other arithmetic: 9.06 us -> none  [the longest x3 8.86 us: advance(): return center + diffusivity * spread - carried]
    dot_general x2 -> x0, matrix products: 7.13 us -> none  [the longest x1 4.43 us: react(): jnp.einsum('rs,ksc->krc', rate_matrix, mixed, precision=lax.Precision.HIG...]
    reduce_sum x1 -> x0, other arithmetic: 3.9 us -> none  [per_device(): average = lax.psum(jnp.sum(flattened, axis=0), 'field') / F]
  transfers between devices with their start and end apart: 9 -> 0, of which waited for: 9 -> 0; matrix products, arithmetic and copies ran while one was open for 7% -> 0% of each run, Pallas kernels for 0% -> 0%
where the time goes in v1:
time: 80.8 us; the launch traced here: 80.5 us
  Pallas kernels  74.6 us (92%)
  local copies, waits for them, and re-layouts  5.92 us (7%)
    pallas_call x1, Pallas kernels, per_device(): pl.pallas_call(functools.partial(kernel, slabs, peers, substeps), out_sha...  74.6 us
    unnamed x3, local copies, waits for them, and re-layouts  5.92 us

profile of v1, /device:TPU:1, one launch (start us, length us, event | category | flops | bytes accessed | tf_op | source)
XLA Modules:
  0.0 80.5 jit_solution(12621404180367512975)
XLA Ops:
  0.0 1.4 %copy.10.noise = f32[4,4,3]{2,1,0:T(4,128)} copy(f32[4,4,3]{1,0,2:T(4,128)} %param.12) | data formatting | bytes 384 | tf_op args[3]
  1.4 1.4 %copy.11.matrix = f32[32,16]{1,0:T(8,128)} copy(f32[32,16]{0,1:T(8,128)} %param.15) | data formatting | bytes 4096 | tf_op args[6]
  2.8 74.6 %shard_map.91 = f32[4,16,4,16,128]{4,3,2,1,0:T(8,128)} custom-call(f32[4,16,4,16,128]{4,3,2,1,0:T(8,128)} %x_hbm.1, f32[3,4,16,128]{3,2,1,0:T(8,128)} %vel.1, f32[4,16,128]{2,1,0:T(8,128)} %diff.1, f32[4,4,3]{2,1,0:T(4,128)} %copy.10.noise, f32[4,16,128]{2,1,0:T(8,128)} %rate.1, f32[4,16,128]{2,1,0:T(8,128)} %vapour.1, f32[32,16]{1,0:T(8,128)} %copy.11.matrix, ...), custom_call_target="tpu_custom_call" | custom-call | tf_op jit(solution)/shard_map/pallas_call | solution.py:323
  77.3 3.2 %copy.13 = f32[4,16,4,16,128]{4,3,2,1,0:T(8,128)} copy(f32[4,16,4,16,128]{4,3,2,1,0:T(8,128)} %shard_map.91) | data formatting | bytes 4194304

commit v2 on v1

--- a/solution.py
+++ b/solution.py
@@ -8,7 +8,7 @@
 from jax.sharding import PartitionSpec as P
 
 GROUP = 2
-LANES = 4
+LANES = 8
 DELAYS = (2, 2, 2, 2, 2, 2, 2)
 ROWS = 8
 
@@ -31,13 +31,16 @@
     return width, [e[2:] for e in sorted(events, key=lambda e: (e[0], e[1]))]
 
 
-def expand(small, row_of, col_of):
-    rows, cols = small.shape
+def expand(small, turned=False):
+    rows, cols = small.shape[::-1] if turned else small.shape
     tall = lax.broadcasted_iota(jnp.int32, (rows * ROWS, rows), 0) // ROWS
     pick_row = (tall == lax.broadcasted_iota(jnp.int32, (rows * ROWS, rows), 1)).astype(jnp.bfloat16)
     wide = lax.broadcasted_iota(jnp.int32, (cols, cols * ROWS), 1) // ROWS
     pick_col = (wide == lax.broadcasted_iota(jnp.int32, (cols, cols * ROWS), 0)).astype(jnp.bfloat16)
-    half = jnp.dot(pick_row, small, preferred_element_type=jnp.float32).astype(jnp.bfloat16)
+    half = lax.dot_general(
+        pick_row, small, (((1,), (1 if turned else 0,)), ((), ())),
+        preferred_element_type=jnp.float32,
+    ).astype(jnp.bfloat16)
     full = jnp.dot(half, pick_col, preferred_element_type=jnp.float32)
     shape = (rows * ROWS, cols * ROWS)
     same = (lax.broadcasted_iota(jnp.int32, shape, 0) % ROWS) == (
@@ -60,7 +63,6 @@
     in_sem, out_sem, hs_sem, hr_sem, rs_sem, rr_sem,
 ):
     fields, species, nx, nz, ny = x_hbm.shape
-    reactions = matrix.shape[0]
     groups = species // GROUP
     bits = peers.bit_length() - 1
     stages = bits + 1
@@ -166,12 +168,12 @@
         planes[x, 5] = 1.0 - 6.0 * d
 
     w_high, w_low = halves(matrix[...])
-    a_high = expand(w_high, ROWS, ROWS)
+    a_high = expand(w_high, True)
     a_one[...] = jnp.concatenate([a_high, a_high], axis=1)
-    a_two[...] = expand(w_low, ROWS, ROWS)
+    a_two[...] = expand(w_low, True)
     s_high, s_low = halves(stoich[...] * pref[...])
-    b_high = expand(s_high, ROWS, ROWS)
-    b_all[...] = jnp.concatenate([b_high, b_high, expand(s_low, ROWS, ROWS)], axis=1)
+    b_high = expand(s_high)
+    b_all[...] = jnp.concatenate([b_high, b_high, expand(s_low)], axis=1)
 
     def exchange(g, stage):
         if stage == 0:
@@ -193,7 +195,7 @@
 
         @pl.loop(0, fields)
         def _(f):
-            shift = [noise[f, k, i] for i in range(3)]
+            shift = [noise[i, f, k] for i in range(3)]
             for x in range(nx):
                 root = planes[x, 3]
                 twice = planes[x, 4]
@@ -352,8 +354,8 @@
                 collective_id=0, has_side_effects=True, vmem_limit_bytes=60 * 1024 * 1024
             ),
         )(
-            fields, velocity, diffusivity, noise, mix_rate, evaporation,
-            rate_matrix, stoich, prefactor.reshape(1, -1),
+            fields, velocity, diffusivity, noise.transpose(2, 0, 1), mix_rate, evaporation,
+            rate_matrix.T, stoich, prefactor.reshape(1, -1),
         )
 
     in_specs = (

time: 80.8 us -> 76 us (0.941)
  local copies, waits for them, and re-layouts: 5.92 us -> 3.16 us
  Pallas kernels: 74.6 us -> 72.7 us
    unnamed x3 -> x1, local copies, waits for them, and re-layouts: 5.92 us -> 3.16 us
    pallas_call x1, Pallas kernels: 74.6 us -> 72.7 us  [per_device(): pl.pallas_call(functools.partial(kernel, slabs, peers, substeps), out_sha...]
where the time goes in v2:
time: 76 us; the launch traced here: 75.8 us
  Pallas kernels  72.7 us (96%)
  local copies, waits for them, and re-layouts  3.16 us (4%)
    pallas_call x1, Pallas kernels, per_device(): pl.pallas_call(functools.partial(kernel, slabs, peers, substeps), out_sha...  72.7 us
    unnamed x1, local copies, waits for them, and re-layouts  3.16 us

profile of v2, /device:TPU:1, one launch (start us, length us, event | category | flops | bytes accessed | tf_op | source)
XLA Modules:
  0.0 75.8 jit_solution(7173698680035100127)
XLA Ops:
  0.0 72.7 %shard_map.91 = f32[4,16,4,16,128]{4,3,2,1,0:T(8,128)} custom-call(f32[4,16,4,16,128]{4,3,2,1,0:T(8,128)} %x_hbm.1, f32[3,4,16,128]{3,2,1,0:T(8,128)} %vel.1, f32[4,16,128]{2,1,0:T(8,128)} %diff.1, f32[3,4,4]{2,1,0:T(4,128)} %bitcast.4, f32[4,16,128]{2,1,0:T(8,128)} %rate.1, f32[4,16,128]{2,1,0:T(8,128)} %vapour.1, f32[16,32]{1,0:T(8,128)} %bitcast.3, ...), custom_call_target="tpu_custom_call" | custom-call | tf_op jit(solution)/shard_map/pallas_call | solution.py:325
  72.7 3.2 %copy.11 = f32[4,16,4,16,128]{4,3,2,1,0:T(8,128)} copy(f32[4,16,4,16,128]{4,3,2,1,0:T(8,128)} %shard_map.91) | data formatting | bytes 4194304
